TPU v7x, 32 devices: a whole 2x2x4 slice. The times are simulated.
32 devices in a mesh: row: 8 (over y, x, core), col: 4 (over z).
Axes of the slice: x: 2, y: 2, z: 4, core: 2. Of those that a mesh axis runs over, the one named last changes fastest.
Arguments:
- pair: bfloat16 [256, 256, 128], P('row', 'col'), may hold values from -6 to 6
- group: bfloat16 [32, 256, 128], P('col', 'row'), may hold values from -6 to 6
- w_query: bfloat16 [128, 128], replicated, may hold values from -0.5 to 0.5
- w_key: bfloat16 [128, 128], replicated, may hold values from -0.5 to 0.5
- w_value: bfloat16 [128, 128], replicated, may hold values from -0.5 to 0.5
- w_gate: bfloat16 [128, 128], replicated, may hold values from -0.5 to 0.5
- w_bias: float32 [128, 4], replicated, may hold values from -40 to 40
- w_out: bfloat16 [128, 128], replicated, may hold values from -0.5 to 0.5
Outputs:
- update: bfloat16 [32, 256, 128], P('col', 'row')
All inputs are finite; a program needn't handle non-finite values.
Results may differ from a plain program's by a relative error of at most 0.012.
Values may be sent and summed in bfloat16 or wider, within the bound.
No kernel may reach another device: no remote copies, remote signals or barrier semaphores. Data moves between devices by JAX's collectives and lax.ppermute only.
A program may use at most 64 MiB of HBM per device.

v0:
```python
import math
import jax
import jax.numpy as jnp
from jax import lax
from jax.sharding import PartitionSpec as P

EPS = 1e-05


def normalize(entries):
    average = jnp.mean(entries, axis=-1, keepdims=True)
    centered = entries - average
    spread = jnp.mean(centered * centered, axis=-1, keepdims=True)
    return centered * lax.rsqrt(spread + EPS)


def per_device(pair, group, w_query, w_key, w_value, w_gate, w_bias, w_out):
    head_count = w_bias.shape[1]
    proj_width = w_query.shape[1]
    head_dim = proj_width // head_count
    query_rows, pair_cols, channels = group.shape
    normed_pair = normalize(pair.astype(jnp.float32))
    bias_local = jnp.einsum("jkc,ch->hjk", normed_pair, w_bias, precision=lax.Precision.HIGHEST)
    bias_panel = lax.all_gather(bias_local, "col", axis=2, tiled=True)
    normed = normalize(group.astype(jnp.float32)).astype(jnp.bfloat16)
    flat_rows = normed.reshape(-1, channels)
    scale = 1.0 / math.sqrt(head_dim)
    query = (jnp.dot(flat_rows, w_query, preferred_element_type=jnp.float32) * scale).astype(
        jnp.bfloat16
    )
    query = query.reshape(query_rows, pair_cols, head_count, head_dim)
    gating = jax.nn.sigmoid(jnp.dot(flat_rows, w_gate, preferred_element_type=jnp.float32))
    gating = gating.reshape(query_rows, pair_cols, head_count, head_dim)
    block_rows = lax.all_gather(normed, "row", axis=1, tiled=True)
    key_count = block_rows.shape[1]
    block_flat = block_rows.reshape(-1, channels)
    key_part = jnp.dot(block_flat, w_key, preferred_element_type=jnp.float32).astype(jnp.bfloat16)
    value_part = jnp.dot(block_flat, w_value, preferred_element_type=jnp.float32).astype(
        jnp.bfloat16
    )
    key_part = key_part.reshape(query_rows, key_count, head_count, head_dim)
    value_part = value_part.reshape(query_rows, key_count, head_count, head_dim)
    run_max = jnp.full((query_rows, head_count, pair_cols), -1e30, jnp.float32)
    scores = (
        jnp.einsum("ijhd,ikhd->ihjk", query, key_part, preferred_element_type=jnp.float32)
        + bias_panel[None]
    )
    new_max = jnp.maximum(run_max, jnp.max(scores, axis=-1))
    weights = jnp.exp(scores - new_max[..., None])
    run_sum = jnp.sum(weights, axis=-1)
    mixture = jnp.einsum(
        "ihjk,ikhd->ijhd",
        weights.astype(jnp.bfloat16),
        value_part,
        preferred_element_type=jnp.float32,
    )
    accumulated = mixture
    run_max, run_sum, accumulated = (new_max, run_sum, accumulated)
    attention = accumulated / jnp.transpose(run_sum, (0, 2, 1))[..., None]
    hidden = (gating * attention).astype(jnp.bfloat16).reshape(-1, proj_width)
    result = jnp.dot(hidden, w_out, preferred_element_type=jnp.float32).astype(jnp.bfloat16)
    return result.reshape(query_rows, pair_cols, channels)


def solution(mesh):
    in_specs = (P("row", "col", None), P("col", "row", None), P(), P(), P(), P(), P(), P())
    out_specs = P("col", "row", None)
    return jax.shard_map(
        per_device, mesh=mesh, in_specs=in_specs, out_specs=out_specs, check_vma=False
    )
```

profile of v0, /device:TPU:0, one launch (start us, length us, event | category | flops | bytes accessed | tf_op | source)
XLA Modules:
  0.0 40.9 jit_solution(7191558274230785309)
XLA Ops:
  0.0 1.0 %convert_reduce_fusion.1 = f32[8,32]{1,0:T(8,128)S(1)} fusion(bf16[8,32,128]{2,1,0:T(8,128)(2,1)} %param.9), kind=kLoop, calls=%fused_computation.30 | loop fusion | flops 65280 | bytes 66560 | tf_op jit(solution)/shard_map/reduce_sum | solution.py:11
  1.0 0.2 fusion.22
  1.4 11.3 %all_gather.6 = bf16[8,256,128]{2,1,0:T(8,128)(2,1)S(1)} all-gather(bf16[8,32,128]{2,1,0:T(8,128)(2,1)S(1)} %fusion.23), channel_id=1, replica_groups=mesh['row'=8,'col'=4] {'row'}, dimensions={1}, use_global_device_ids=true | all-gather | bytes 589824 | tf_op jit(solution)/shard_map/all_gather | solution.py:34
  12.7 0.3 convolution_convert_fusion
  13.0 0.2 copy.23
  13.4 0.6 %copy-done.3 = bf16[128,128]{1,0:T(8,128)(2,1)S(1)} copy-done((bf16[128,128]{1,0:T(8,128)(2,1)S(1)}, bf16[128,128]{1,0:T(8,128)(2,1)}, u32[]{:S(2)}) %copy-start.3) | copy-done | bytes 32792
  14.3 0.3 convert_reduce_fusion
  14.7 0.6 %fusion.9 = f32[32,64]{1,0:T(8,128)S(1)} fusion(bf16[32,64,128]{2,1,0:T(8,128)(2,1)S(1)} %copy-done.1, f32[32,64]{1,0:T(8,128)S(1)} %broadcast_multiply_fusion), kind=kLoop, calls=%fused_computation.19 | loop fusion | flops 1046528 | bytes 540672 | tf_op jit(solution)/shard_map/reduce_sum | solution.py:13
  15.4 0.7 %copy-done.7 = f32[128,4]{0,1:T(4,128)S(1)} copy-done((f32[128,4]{0,1:T(4,128)S(1)}, f32[128,4]{0,1:T(4,128)}, u32[]{:S(2)}) %copy-start.7) | copy-done | bytes 2072
  16.0 2.9 %convolution_bitcast_fusion.1 = f32[4,32,64]{2,0,1:T(4,128)S(1)} fusion(bf16[32,64,128]{2,1,0:T(8,128)(2,1)S(1)} %copy-done.1, f32[32,64]{1,0:T(8,128)S(1)} %add_rsqrt_fusion, f32[32,64]{1,0:T(8,128)S(1)} %broadcast_multiply_fusion, f32[128,4]{0,1:T(4,128)S(1)} %copy-done.7), kind=kOutput, calls=%fused_computation.18 | convolution fusion | flops 13369344 | bytes 575488 | tf_op jit(solution)/shard_map/jkc,ch->hjk/dot_general | solution.py:23
  19.1 16.3 %all_gather.7 = f32[4,32,256]{1,0,2:T(4,128)S(1)} all-gather(f32[4,32,64]{1,0,2:T(4,128)S(1)} %copy.26), channel_id=1, replica_groups=mesh['row'=8,'col'=4] {'col'}, dimensions={2}, use_global_device_ids=true | all-gather | bytes 163840 | tf_op jit(solution)/shard_map/all_gather | solution.py:24
  35.4 0.2 copy.27
  35.6 0.4 fusion.25
  36.0 0.4 %fusion.11 = f32[8,4,32]{2,1,0:T(4,128)S(1)} fusion(f32[8,4,32,256]{3,2,1,0:T(8,128)S(1)} %get-tuple-element.6, f32[8,4,32]{2,1,0:T(4,128)S(1)} %broadcast_maximum_fusion), kind=kLoop, calls=%fused_computation.21 | loop fusion | flops 523264 | bytes 1056768 | tf_op jit(solution)/shard_map/reduce_sum | solution.py:50
  36.4 0.3 copy-done.4
  36.8 0.3 convolution_convert_fusion.1
  37.0 0.2 copy.22
  37.4 0.6 %copy-done.6 = bf16[128,128]{1,0:T(8,128)(2,1)S(1)} copy-done((bf16[128,128]{1,0:T(8,128)(2,1)S(1)}, bf16[128,128]{1,0:T(8,128)(2,1)}, u32[]{:S(2)}) %copy-start.6) | copy-done | bytes 32792
  38.2 0.3 reshape.54
  38.5 0.2 copy.29
  38.7 0.4 fusion.4
  39.3 0.2 reshape.59
  39.5 0.6 %copy-done.5 = bf16[128,128]{1,0:T(8,128)(2,1)S(1)} copy-done((bf16[128,128]{1,0:T(8,128)(2,1)S(1)}, bf16[128,128]{1,0:T(8,128)(2,1)}, u32[]{:S(2)}) %copy-start.5) | copy-done | bytes 32792
  40.0 0.8 %convolution_convert_fusion.2 = bf16[256,128]{1,0:T(8,128)(2,1)} fusion(bf16[256,128]{0,1:T(8,128)(2,1)S(1)} %reshape.59, bf16[128,128]{1,0:T(8,128)(2,1)S(1)} %copy-done.5), kind=kOutput, calls=%fused_computation.16 | convolution fusion | flops 8421376 | bytes 163840 | tf_op jit(solution)/shard_map/dot_general | solution.py:61
  (24 shorter events, 1.2 us)
Async XLA Ops:
  0.0 12.7 %copy-start = (bf16[128,128]{1,0:T(8,128)(2,1)S(1)}, bf16[128,128]{1,0:T(8,128)(2,1)}, u32[]{:S(2)}) copy-start(bf16[128,128]{1,0:T(8,128)(2,1)} %param.11) | copy-start | bytes 98308
  0.0 1.0 %copy-start.2 = (bf16[8,32,128]{2,1,0:T(8,128)(2,1)S(1)}, bf16[8,32,128]{2,1,0:T(8,128)(2,1)}, u32[]{:S(2)}) copy-start(bf16[8,32,128]{2,1,0:T(8,128)(2,1)} %param.9) | copy-start | bytes 196612
  13.2 0.8 %copy-start.3 = (bf16[128,128]{1,0:T(8,128)(2,1)S(1)}, bf16[128,128]{1,0:T(8,128)(2,1)}, u32[]{:S(2)}) copy-start(bf16[128,128]{1,0:T(8,128)(2,1)} %param.10) | copy-start | bytes 98308
  13.2 1.1 %copy-start.1 = (bf16[32,64,128]{2,1,0:T(8,128)(2,1)S(1)}, bf16[32,64,128]{2,1,0:T(8,128)(2,1)}, u32[]{:S(2)}) copy-start(bf16[32,64,128]{2,1,0:T(8,128)(2,1)} %param.8) | copy-start | bytes 1572868
  15.3 0.7 %copy-start.7 = (f32[128,4]{0,1:T(4,128)S(1)}, f32[128,4]{0,1:T(4,128)}, u32[]{:S(2)}) copy-start(f32[128,4]{0,1:T(4,128)} %param.14) | copy-start | bytes 6148
  36.0 0.8 %copy-start.4 = (bf16[128,128]{1,0:T(8,128)(2,1)S(1)}, bf16[128,128]{1,0:T(8,128)(2,1)}, u32[]{:S(2)}) copy-start(bf16[128,128]{1,0:T(8,128)(2,1)} %param.12) | copy-start | bytes 98308
  37.3 0.8 %copy-start.6 = (bf16[128,128]{1,0:T(8,128)(2,1)S(1)}, bf16[128,128]{1,0:T(8,128)(2,1)}, u32[]{:S(2)}) copy-start(bf16[128,128]{1,0:T(8,128)(2,1)} %param.13) | copy-start | bytes 98308
  39.3 0.8 %copy-start.5 = (bf16[128,128]{1,0:T(8,128)(2,1)S(1)}, bf16[128,128]{1,0:T(8,128)(2,1)}, u32[]{:S(2)}) copy-start(bf16[128,128]{1,0:T(8,128)(2,1)} %param.15) | copy-start | bytes 98308
where the time goes:
time: 41.3 us; the launch traced here: 40.9 us
  blocking collectives  27.7 us (67%)
  matrix products  5.42 us (13%)
  local copies, waits for them, and re-layouts  4.77 us (12%)
  other arithmetic  2.76 us (7%)
    all_gather x1, blocking collectives, per_device(): bias_panel = lax.all_gather(bias_local, 'col', axis=2, tiled=True)  16.3 us
    all_gather x1, blocking collectives, per_device(): block_rows = lax.all_gather(normed, 'row', axis=1, tiled=True)  11.3 us
    unnamed x18, local copies, waits for them, and re-layouts  3.06 us
    dot_general x1, matrix products, per_device(): jnp.einsum('jkc,ch->hjk', normed_pair, w_bias, precision=lax.Precision.HI...  2.93 us
    reduce_sum x2, other arithmetic, normalize(): average = jnp.mean(entries, axis=-1, keepdims=True)  1.35 us

commit v1 on v0

--- a/solution.py
+++ b/solution.py
@@ -21,7 +21,7 @@
     query_rows, pair_cols, channels = group.shape
     normed_pair = normalize(pair.astype(jnp.float32))
     bias_local = jnp.einsum("jkc,ch->hjk", normed_pair, w_bias, precision=lax.Precision.HIGHEST)
-    bias_panel = lax.all_gather(bias_local, "col", axis=2, tiled=True)
+    bias_panel = jnp.concatenate(lax.all_gather(bias_local, "col"), axis=2)
     normed = normalize(group.astype(jnp.float32)).astype(jnp.bfloat16)
     flat_rows = normed.reshape(-1, channels)
     scale = 1.0 / math.sqrt(head_dim)

time: 41.3 us -> 39.1 us (0.947)
  blocking collectives: 27.7 us -> 25.4 us
    all_gather x1, blocking collectives: 16.3 us -> 14.1 us  [per_device(): bias_panel = jnp.concatenate(lax.all_gather(bias_local, 'col'), axis=2)]
where the time goes in v1:
time: 39.1 us; the launch traced here: 38.7 us
  blocking collectives  25.4 us (65%)
  matrix products  5.43 us (14%)
  local copies, waits for them, and re-layouts  4.85 us (12%)
  other arithmetic  2.76 us (7%)
    all_gather x1, blocking collectives, per_device(): bias_panel = jnp.concatenate(lax.all_gather(bias_local, 'col'), axis=2)  14.1 us
    all_gather x1, blocking collectives, per_device(): block_rows = lax.all_gather(normed, 'row', axis=1, tiled=True)  11.3 us
    unnamed x18, local copies, waits for them, and re-layouts  3.06 us
    dot_general x1, matrix products, per_device(): jnp.einsum('jkc,ch->hjk', normed_pair, w_bias, precision=lax.Precision.HI...  2.93 us
    reduce_sum x2, other arithmetic, normalize(): average = jnp.mean(entries, axis=-1, keepdims=True)  1.35 us
    dot_general x1, matrix products, per_device(): jnp.dot(hidden, w_out, preferred_element_type=jnp.float32)  0.82 us
    reduce_sum x2, other arithmetic, normalize(): spread = jnp.mean(centered * centered, axis=-1, keepdims=True)  0.82 us

profile of v1, /device:TPU:0, one launch (start us, length us, event | category | flops | bytes accessed | tf_op | source)
XLA Modules:
  0.0 38.7 jit_solution(10114434642766362012)
XLA Ops:
  0.0 1.0 %convert_reduce_fusion.1 = f32[8,32]{1,0:T(8,128)S(1)} fusion(bf16[8,32,128]{2,1,0:T(8,128)(2,1)} %param.9), kind=kLoop, calls=%fused_computation.30 | loop fusion | flops 65280 | bytes 66560 | tf_op jit(solution)/shard_map/reduce_sum | solution.py:11
  1.0 0.2 fusion.22
  1.4 11.3 %all_gather.9 = bf16[8,256,128]{2,1,0:T(8,128)(2,1)S(1)} all-gather(bf16[8,32,128]{2,1,0:T(8,128)(2,1)S(1)} %fusion.23), channel_id=1, replica_groups=mesh['row'=8,'col'=4] {'row'}, dimensions={1}, use_global_device_ids=true | all-gather | bytes 589824 | tf_op jit(solution)/shard_map/all_gather | solution.py:34
  12.7 0.3 convolution_convert_fusion
  13.0 0.2 copy.23
  13.4 0.6 %copy-done.3 = bf16[128,128]{1,0:T(8,128)(2,1)S(1)} copy-done((bf16[128,128]{1,0:T(8,128)(2,1)S(1)}, bf16[128,128]{1,0:T(8,128)(2,1)}, u32[]{:S(2)}) %copy-start.3) | copy-done | bytes 32792
  14.3 0.3 convert_reduce_fusion
  14.7 0.6 %fusion.9 = f32[32,64]{1,0:T(8,128)S(1)} fusion(bf16[32,64,128]{2,1,0:T(8,128)(2,1)S(1)} %copy-done.1, f32[32,64]{1,0:T(8,128)S(1)} %broadcast_multiply_fusion), kind=kLoop, calls=%fused_computation.19 | loop fusion | flops 1046528 | bytes 540672 | tf_op jit(solution)/shard_map/reduce_sum | solution.py:13
  15.4 0.7 %copy-done.7 = f32[128,4]{0,1:T(4,128)S(1)} copy-done((f32[128,4]{0,1:T(4,128)S(1)}, f32[128,4]{0,1:T(4,128)}, u32[]{:S(2)}) %copy-start.7) | copy-done | bytes 2072
  16.0 2.9 %convolution_bitcast_fusion.1 = f32[4,32,64]{2,0,1:T(4,128)S(1)} fusion(bf16[32,64,128]{2,1,0:T(8,128)(2,1)S(1)} %copy-done.1, f32[32,64]{1,0:T(8,128)S(1)} %add_rsqrt_fusion, f32[32,64]{1,0:T(8,128)S(1)} %broadcast_multiply_fusion, f32[128,4]{0,1:T(4,128)S(1)} %copy-done.7), kind=kOutput, calls=%fused_computation.18 | convolution fusion | flops 13369344 | bytes 575488 | tf_op jit(solution)/shard_map/jkc,ch->hjk/dot_general | solution.py:23
  19.0 14.1 %all-gather = f32[16,32,64]{2,1,0:T(8,128)S(1)} all-gather(f32[4,32,64]{2,1,0:T(8,128)S(1)} %copy.26), channel_id=2, replica_groups=mesh['row'=8,'col'=4] {'col'}, dimensions={0}, use_global_device_ids=true | all-gather | bytes 163840 | tf_op jit(solution)/shard_map/all_gather | solution.py:24
  33.2 0.2 add.40
  33.4 0.4 %fusion.25 = (f32[8,4,32]{2,1,0:T(4,128)S(1)}, f32[8,4,32,256]{3,2,1,0:T(8,128)S(1)}) fusion(f32[4,32,256]{2,1,0:T(8,128)S(1)} %add.40, bf16[8,256,4,32]{1,0,3,2:T(8,128)(2,1)S(1)} %bitcast.48, bf16[8,32,4,32]{3,2,1,0:T(4,128)(2,1)S(1)} %reshape.60), kind=kOutput, calls=%fused_computation.41 | convolution fusion | flops 17300480 | bytes 1773568 | tf_op jit(solution)/shard_map/ijhd,ikhd->ihjk/dot_general | solution.py:45
  33.9 0.4 %fusion.11 = f32[8,4,32]{2,1,0:T(4,128)S(1)} fusion(f32[8,4,32,256]{3,2,1,0:T(8,128)S(1)} %get-tuple-element.6, f32[8,4,32]{2,1,0:T(4,128)S(1)} %broadcast_maximum_fusion), kind=kLoop, calls=%fused_computation.21 | loop fusion | flops 523264 | bytes 1056768 | tf_op jit(solution)/shard_map/reduce_sum | solution.py:50
  34.3 0.3 copy-done.4
  34.6 0.3 convolution_convert_fusion.1
  34.9 0.2 copy.22
  35.2 0.6 %copy-done.6 = bf16[128,128]{1,0:T(8,128)(2,1)S(1)} copy-done((bf16[128,128]{1,0:T(8,128)(2,1)S(1)}, bf16[128,128]{1,0:T(8,128)(2,1)}, u32[]{:S(2)}) %copy-start.6) | copy-done | bytes 32792
  36.1 0.3 reshape.57
  36.3 0.2 copy.29
  36.5 0.4 %fusion.4 = bf16[8,32,4,32]{1,3,2,0:T(8,128)(2,1)S(1)} fusion(f32[8,32,4,32]{1,3,2,0:T(8,128)S(1)} %copy.29, f32[8,4,32,256]{3,2,1,0:T(8,128)S(1)} %get-tuple-element.6, bf16[8,256,4,32]{1,0,3,2:T(8,128)(2,1)S(1)} %bitcast.52, f32[8,4,32]{2,1,0:T(4,128)S(1)} %broadcast_maximum_fusion, f32[8,32,4]{1,2,0:T(4,128)S(1)} %bitcast.53), kind=kOutput, calls=%fused_computation.10 | convolution fusion | flops 17399808 | bytes 1777664 | tf_op jit(solution)/shard_map/ihjk,ikhd->ijhd/dot_general | solution.py:51
  37.1 0.2 reshape.63
  37.3 0.6 %copy-done.5 = bf16[128,128]{1,0:T(8,128)(2,1)S(1)} copy-done((bf16[128,128]{1,0:T(8,128)(2,1)S(1)}, bf16[128,128]{1,0:T(8,128)(2,1)}, u32[]{:S(2)}) %copy-start.5) | copy-done | bytes 32792
  37.9 0.8 %convolution_convert_fusion.2 = bf16[256,128]{1,0:T(8,128)(2,1)} fusion(bf16[256,128]{0,1:T(8,128)(2,1)S(1)} %reshape.63, bf16[128,128]{1,0:T(8,128)(2,1)S(1)} %copy-done.5), kind=kOutput, calls=%fused_computation.16 | convolution fusion | flops 8421376 | bytes 163840 | tf_op jit(solution)/shard_map/dot_general | solution.py:61
  (25 shorter events, 1.3 us)
Async XLA Ops:
  0.0 12.7 %copy-start = (bf16[128,128]{1,0:T(8,128)(2,1)S(1)}, bf16[128,128]{1,0:T(8,128)(2,1)}, u32[]{:S(2)}) copy-start(bf16[128,128]{1,0:T(8,128)(2,1)} %param.11) | copy-start | bytes 98308
  0.0 1.0 %copy-start.2 = (bf16[8,32,128]{2,1,0:T(8,128)(2,1)S(1)}, bf16[8,32,128]{2,1,0:T(8,128)(2,1)}, u32[]{:S(2)}) copy-start(bf16[8,32,128]{2,1,0:T(8,128)(2,1)} %param.9) | copy-start | bytes 196612
  13.2 0.8 %copy-start.3 = (bf16[128,128]{1,0:T(8,128)(2,1)S(1)}, bf16[128,128]{1,0:T(8,128)(2,1)}, u32[]{:S(2)}) copy-start(bf16[128,128]{1,0:T(8,128)(2,1)} %param.10) | copy-start | bytes 98308
  13.2 1.1 %copy-start.1 = (bf16[32,64,128]{2,1,0:T(8,128)(2,1)S(1)}, bf16[32,64,128]{2,1,0:T(8,128)(2,1)}, u32[]{:S(2)}) copy-start(bf16[32,64,128]{2,1,0:T(8,128)(2,1)} %param.8) | copy-start | bytes 1572868
  15.3 0.7 %copy-start.7 = (f32[128,4]{0,1:T(4,128)S(1)}, f32[128,4]{0,1:T(4,128)}, u32[]{:S(2)}) copy-start(f32[128,4]{0,1:T(4,128)} %param.14) | copy-start | bytes 6148
  33.9 0.8 %copy-start.4 = (bf16[128,128]{1,0:T(8,128)(2,1)S(1)}, bf16[128,128]{1,0:T(8,128)(2,1)}, u32[]{:S(2)}) copy-start(bf16[128,128]{1,0:T(8,128)(2,1)} %param.12) | copy-start | bytes 98308
  35.1 0.8 %copy-start.6 = (bf16[128,128]{1,0:T(8,128)(2,1)S(1)}, bf16[128,128]{1,0:T(8,128)(2,1)}, u32[]{:S(2)}) copy-start(bf16[128,128]{1,0:T(8,128)(2,1)} %param.13) | copy-start | bytes 98308
  37.1 0.8 %copy-start.5 = (bf16[128,128]{1,0:T(8,128)(2,1)S(1)}, bf16[128,128]{1,0:T(8,128)(2,1)}, u32[]{:S(2)}) copy-start(bf16[128,128]{1,0:T(8,128)(2,1)} %param.15) | copy-start | bytes 98308
